TPU v7x, 32 devices: a whole 2x2x4 slice. The times are simulated.
32 devices in a mesh: rep: 2 (over y), ep: 16 (over z, x, core).
Axes of the slice: x: 2, y: 2, z: 4, core: 2. Of those that a mesh axis runs over, the one named last changes fastest.
Arguments:
- cache_kv: bfloat16 [64, 2048, 576], P(('rep', 'ep')), parts along dimension 0, may hold values from -6 to 6
- new_kv: bfloat16 [64, 2, 576], P(('rep', 'ep')), parts along dimension 0, may hold values from -6 to 6
- queries: bfloat16 [64, 2, 64, 576], P(('rep', 'ep')), parts along dimension 0, may hold values from -256 to 256
- lengths: int32 [64], P(('rep', 'ep')), parts along dimension 0, may hold values from 256 to 2048
- resid: bfloat16 [64, 2, 7168], P(('rep', 'ep')), parts along dimension 0, may hold values from -18 to 18
- value_up: bfloat16 [512, 8192], P(None, 'ep'), may hold values from -1.5 to 1.5
- out_proj: bfloat16 [8192, 7168], P('ep'), may hold values from -0.09375 to 0.09375
- norm_gain: bfloat16 [7168], replicated, may hold values from 0.25 to 1.75
- router: bfloat16 [7168, 16], replicated, may hold values from -0.0625 to 0.0625
- expert_ids: int32 [64, 2, 8], P(('rep', 'ep')), parts along dimension 0, may hold values from 0 to 15, as said below
- slots: int32 [64, 2, 8], P(('rep', 'ep')), parts along dimension 0, may hold values from 0 to 3, as said below
- w_gate: bfloat16 [7168, 16384], P(None, 'ep'), may hold values from -0.0625 to 0.0625
- w_up: bfloat16 [7168, 16384], P(None, 'ep'), may hold values from -0.0625 to 0.0625
- w_down: bfloat16 [16384, 7168], P('ep'), may hold values from -0.1875 to 0.1875
Outputs:
- mixed: bfloat16 [64, 2, 7168], P(('rep', 'ep')), parts along dimension 0
There are 2 independent parts, one for each index of `rep`. A program takes and returns all parts, laid end to end along the dimension named above; an argument that names none is the same for every part. Nothing has to cross between parts.
Inputs may be any that keep to these rules, and one draw needn't show every extreme that they name: `expert_ids`: each row names 8 different experts. In each aligned block of 4 rows (the rows of one device), the rows that name the same expert carry the distinct slots 0 up to their number minus one for it; in every block some expert is named by all 4 rows.
All inputs are finite; a program needn't handle non-finite values.
Results may differ from a plain program's by a relative error of at most 0.0065.
Values may be sent and summed in bfloat16 or wider, within the bound.
A program may use at most 128 MiB of HBM per device.

v0:
```python
import functools
import math

import jax
import jax.numpy as jnp
from jax import lax
from jax.experimental import pallas as pl
from jax.experimental.pallas import tpu as pltpu
from jax.sharding import PartitionSpec as P

D = 7168
H = 64
LAT = 512
VH = 128
EXPERTS = 16
TOP = 8
CAP = 2
QK = 192


route_scale = 2.827
norm_eps = 1e-06


F32 = jnp.float32
BF16 = jnp.bfloat16
CORES = 2
LINE = 4
CHUNKS = 4


def loop(count, step, start=0):
    lax.fori_loop(start, count, lambda i, carry: (step(i), carry)[1], 0)


def layer_kernel(
    n,
    len_ref,
    new_ref,
    gain_ref,
    router_ref,
    ids_ref,
    slots_ref,
    cache_hbm,
    query_hbm,
    resid_hbm,
    vu_hbm,
    op_hbm,
    wg_hbm,
    wu_hbm,
    wd_hbm,
    out_ref,
    vu,
    op,
    wg,
    wu,
    wd,
    keys,
    fresh,
    query,
    resid,
    ctx32,
    ctx_ref,
    ctx_in,
    rows32,
    acc32,
    gate_acc,
    up_acc,
    hid,
    part,
    pair_sum,
    line_sum,
    in_core0,
    in_mid0,
    in_line0,
    in_core1,
    in_mid1,
    in_line1,
    gathered,
    share_out,
    share_in,
    share_all,
    w_sem,
    key_sem,
    ctx_send,
    ctx_recv,
    share_send,
    share_recv,
    core_sem,
    mid_send,
    mid_recv,
    line_send,
    line_recv,
):
    me = lax.axis_index("ep")
    mids = n // (CORES * LINE)
    c = me % CORES
    b = (me // CORES) % mids
    a = me // (CORES * mids)
    seqs, steps, width = resid.shape
    toks = seqs * steps
    part_w = width // CHUNKS
    rows_each = ctx_ref.shape[1]
    heads_per = rows_each // toks
    value_cols = vu.shape[1]
    total = n * toks
    fan = CORES * mids
    per = 8 // toks

    def stack(ref, block, rows):
        group = 8 // rows

        def put(g):
            tile = jnp.concatenate([block(g * group + h) for h in range(group)], axis=0)
            ref[pl.ds(pl.multiple_of(g * 8, 8), 8), :] = tile

        loop(n // group, put)

    def dev(aa, bb, cc):
        return (aa * mids + bb) * CORES + cc

    def send(src, dst, s_sem, r_sem, target):
        return pltpu.make_async_remote_copy(
            src_ref=src,
            dst_ref=dst,
            send_sem=s_sem,
            recv_sem=r_sem,
            device_id={"ep": target},
            device_id_type=pl.DeviceIdType.MESH,
        )

    def cols(ch):
        return pl.ds(pl.multiple_of(ch * part_w, part_w), part_w)

    def op_copy(ch):
        return pltpu.make_async_copy(op_hbm.at[:, cols(ch)], op.at[ch], w_sem.at[0, ch])

    def wg_copy(ch):
        return pltpu.make_async_copy(wg_hbm.at[cols(ch), :], wg.at[ch], w_sem.at[1, ch])

    def wu_copy(ch):
        return pltpu.make_async_copy(wu_hbm.at[cols(ch), :], wu.at[ch], w_sem.at[2, ch])

    def wd_copy(ch):
        return pltpu.make_async_copy(wd_hbm.at[:, cols(ch)], wd.at[ch], w_sem.at[3, ch])

    vu_copy = pltpu.make_async_copy(vu_hbm, vu, w_sem.at[4, 0])
    resid_copy = pltpu.make_async_copy(resid_hbm, resid, w_sem.at[4, 1])
    cache_len = cache_hbm.shape[2]

    def key_copy(q):
        return pltpu.make_async_copy(cache_hbm.at[q], keys.at[q], key_sem.at[0, q])

    def query_copy(q):
        return pltpu.make_async_copy(query_hbm.at[q], query.at[q], key_sem.at[1, q])

    for q in range(seqs):
        query_copy(q).start()
        key_copy(q).start()
    vu_copy.start()
    resid_copy.start()

    barrier = pltpu.get_barrier_semaphore()

    def greet(i):
        pl.semaphore_signal(
            barrier,
            inc=1,
            device_id={"ep": (me + i) % n},
            device_id_type=pl.DeviceIdType.MESH,
        )

    loop(n, greet, 1)
    loop(CHUNKS, lambda ch: op_copy(ch).start())

    def start_ffn(ch):
        wg_copy(ch).start()
        wu_copy(ch).start()

    loop(CHUNKS, start_ffn)
    loop(CHUNKS, lambda ch: wd_copy(ch).start())

    rows_q, span_new = query.shape[1], fresh.shape[1]
    heads = rows_q // steps
    score_scale = 1.0 / math.sqrt(QK)
    fresh[...] = jnp.zeros_like(fresh)
    for q in range(seqs):
        fresh[q, :steps, :] = new_ref[q]
    place = lax.broadcasted_iota(jnp.int32, (rows_q, cache_len), 1)
    newer = lax.broadcasted_iota(jnp.int32, (rows_q, span_new), 1) <= (
        lax.broadcasted_iota(jnp.int32, (rows_q, span_new), 0) // heads
    )
    for q in range(seqs):
        query_copy(q).wait()
        key_copy(q).wait()
        old = jnp.dot(query[q], keys[q], preferred_element_type=F32) * score_scale
        old = jnp.where(place < len_ref[q], old, -jnp.inf)
        new = lax.dot_general(
            query[q], fresh[q], (((1,), (1,)), ((), ())), preferred_element_type=F32
        )
        new = jnp.where(newer, new * score_scale, -jnp.inf)
        peak = jnp.maximum(
            jnp.max(old, axis=-1, keepdims=True), jnp.max(new, axis=-1, keepdims=True)
        )
        old = jnp.exp(old - peak)
        new = jnp.exp(new - peak)
        inverse = 1.0 / (
            jnp.sum(old, axis=-1, keepdims=True) + jnp.sum(new, axis=-1, keepdims=True)
        )
        ctx32[q] = lax.dot_general(
            (old * inverse).astype(BF16),
            keys[q, :LAT, :],
            (((1,), (1,)), ((), ())),
            preferred_element_type=F32,
        ) + jnp.dot(
            (new * inverse).astype(BF16), fresh[q, :, :LAT], preferred_element_type=F32
        )
    for j in range(n):
        first = (j * value_cols) // VH
        rows = [
            ctx32[q, t * heads + first : t * heads + first + heads_per, :]
            for q in range(seqs)
            for t in range(steps)
        ]
        ctx_ref[j] = jnp.concatenate(rows, axis=0).astype(BF16)
    pl.semaphore_wait(barrier, n - 1)

    def ctx_copy(i):
        to = (me + i) % n
        return send(ctx_ref.at[to], ctx_in.at[me], ctx_send.at[to], ctx_recv.at[me], to)

    def ctx_arrival(i):
        frm = (me + i) % n
        return send(ctx_ref.at[frm], ctx_in.at[frm], ctx_send.at[frm], ctx_recv.at[frm], frm)

    loop(n, lambda i: ctx_copy(i).start(), 1)

    lane = lax.broadcasted_iota(jnp.int32, (toks, EXPERTS), 1)
    named = jnp.zeros((toks, EXPERTS), F32)
    kept = jnp.zeros((toks, EXPERTS), F32)
    for k in range(TOP):
        hit = jnp.where(ids_ref[:, k : k + 1] == lane, 1.0, 0.0)
        named = named + hit
        kept = kept + jnp.where(slots_ref[:, k : k + 1] < CAP, hit, 0.0)

    ctx_in[me] = ctx_ref[me]
    vu_copy.wait()
    loop(n, lambda i: ctx_arrival(i).wait_recv(), 1)

    if rows_each % 16 == 0:
        head_rows = ctx_in[...].reshape(n * rows_each, LAT)
    else:

        stack(rows32, lambda i: ctx_in[i].astype(F32), rows_each)
        head_rows = rows32[...].astype(BF16)
    values = jnp.dot(head_rows, vu[...], preferred_element_type=F32)
    if heads_per > 1:
        shape = (n * rows_each, value_cols)
        row_head = lax.broadcasted_iota(jnp.int32, shape, 0) % heads_per
        col_head = lax.broadcasted_iota(jnp.int32, shape, 1) // (value_cols // heads_per)
        values = jnp.where(row_head == col_head, values, 0.0).astype(BF16)
        shape = (total, n * rows_each)
        row_tok = lax.broadcasted_iota(jnp.int32, shape, 1) // heads_per
        fold = jnp.where(row_tok == lax.broadcasted_iota(jnp.int32, shape, 0), 1.0, 0.0)
        values = jnp.dot(fold.astype(BF16), values, preferred_element_type=F32)
    values = values.astype(BF16)

    def reduce_scatter(which, produce, finish):
        in_core, in_mid, in_line = (
            (in_core0, in_mid0, in_line0) if which == 0 else (in_core1, in_mid1, in_line1)
        )

        def core_copy(ch):
            return send(
                part.at[ch, 1 - c],
                in_core.at[ch],
                core_sem.at[which, 0, ch],
                core_sem.at[which, 1, ch],
                dev(a, b, 1 - c),
            )

        def mid_copy(ch, i):
            bb = (b + i) % mids
            return send(
                pair_sum.at[ch, bb],
                in_mid.at[ch, b],
                mid_send.at[which, ch, bb],
                mid_recv.at[which, ch, b],
                dev(a, bb, c),
            )

        def mid_arrival(ch, bb):
            return send(
                pair_sum.at[ch, bb],
                in_mid.at[ch, bb],
                mid_send.at[which, ch, bb],
                mid_recv.at[which, ch, bb],
                dev(a, bb, c),
            )

        def line_copy(ch, i):
            aa = (a + i) % LINE
            return send(
                line_sum.at[ch, aa],
                in_line.at[ch, a],
                line_send.at[which, ch, aa],
                line_recv.at[which, ch, a],
                dev(aa, b, c),
            )

        def line_arrival(ch, aa):
            return send(
                line_sum.at[ch, aa],
                in_line.at[ch, aa],
                line_send.at[which, ch, aa],
                line_recv.at[which, ch, aa],
                dev(aa, b, c),
            )

        def stage1(ch):
            acc32[...] = produce(ch)

            def spread(g):
                tile = acc32[pl.ds(pl.multiple_of(g * 8, 8), 8), :]
                for h in range(per):
                    d = g * per + h
                    part[ch, d % CORES, (d // CORES) % mids, d // fan] = tile[
                        h * toks : (h + 1) * toks
                    ].astype(BF16)

            loop(n // per, spread)
            core_copy(ch).start()

        def stage2(ch):
            core_copy(ch).wait_recv()

            def add_pair(k):
                bb, aa = k // LINE, k % LINE
                pair_sum[ch, bb, aa] = (
                    part[ch, c, bb, aa].astype(F32) + in_core[ch, bb, aa].astype(F32)
                ).astype(BF16)

            loop(mids * LINE, add_pair)
            loop(mids, lambda i: mid_copy(ch, i).start(), 1)

        def stage3(ch):
            loop(mids, lambda i: mid_arrival(ch, (b + i) % mids).wait_recv(), 1)

            def add_mid(aa):
                acc = pair_sum[ch, b, aa].astype(F32)
                acc = lax.fori_loop(
                    1, mids, lambda i, t: t + in_mid[ch, (b + i) % mids, aa].astype(F32), acc
                )
                line_sum[ch, aa] = acc.astype(BF16)

            loop(LINE, add_mid)
            loop(LINE, lambda i: line_copy(ch, i).start(), 1)

        def stage4(ch):
            acc = line_sum[ch, a].astype(F32)
            for i in range(1, LINE):
                aa = (a + i) % LINE
                line_arrival(ch, aa).wait_recv()
                acc = acc + in_line[ch, aa].astype(F32)
            finish(ch, acc)

        def step(t):
            for delay, stage in enumerate((stage1, stage2, stage3, stage4)):
                pl.when((t >= delay) & (t < CHUNKS + delay))(
                    functools.partial(stage, t - delay)
                )

        loop(CHUNKS + 3, step)

        def drain(ch):
            core_copy(ch).wait_send()
            loop(mids, lambda i: mid_copy(ch, i).wait_send(), 1)
            loop(LINE, lambda i: line_copy(ch, i).wait_send(), 1)

        loop(CHUNKS, drain)

    def attended_part(ch):
        op_copy(ch).wait()
        return jnp.dot(values, op[ch], preferred_element_type=F32)

    def keep_hidden(ch, acc):
        rows = [resid[q, :, cols(ch)].astype(F32) for q in range(seqs)]
        hid[ch] = acc + jnp.concatenate(rows, axis=0)

    resid_copy.wait()
    reduce_scatter(0, attended_part, keep_hidden)

    square = jnp.zeros((toks, 1), F32)
    for ch in range(CHUNKS):
        square = square + jnp.sum(hid[ch] * hid[ch], axis=-1, keepdims=True)
    scale = lax.rsqrt(square / width + norm_eps)

    def leg_line(ch, i):
        aa = (a + i) % LINE
        blk = gathered.at[ch, c, b, a]
        return send(blk, blk, line_send.at[2, ch, aa], line_recv.at[2, ch, a], dev(aa, b, c))

    def leg_line_arrival(ch, aa):
        blk = gathered.at[ch, c, b, aa]
        return send(blk, blk, line_send.at[2, ch, aa], line_recv.at[2, ch, aa], dev(aa, b, c))

    def leg_mid(ch, i):
        bb = (b + i) % mids
        blk = gathered.at[ch, c, b]
        return send(blk, blk, mid_send.at[2, ch, bb], mid_recv.at[2, ch, b], dev(a, bb, c))

    def leg_mid_arrival(ch, bb):
        blk = gathered.at[ch, c, bb]
        return send(blk, blk, mid_send.at[2, ch, bb], mid_recv.at[2, ch, bb], dev(a, bb, c))

    def leg_core(ch):
        blk = gathered.at[ch, c]
        return send(
            blk, blk, core_sem.at[2, 0, ch], core_sem.at[2, 1, ch], dev(a, b, 1 - c)
        )

    def leg_core_arrival(ch):
        blk = gathered.at[ch, 1 - c]
        return send(
            blk, blk, core_sem.at[2, 0, ch], core_sem.at[2, 1, ch], dev(a, b, 1 - c)
        )

    logits = jnp.zeros((toks, EXPERTS), F32)
    for ch in range(CHUNKS):
        span = slice(ch * part_w, (ch + 1) * part_w)
        normed = (hid[ch] * scale * gain_ref[:, span].astype(F32)).astype(BF16)
        gathered[ch, c, b, a] = normed
        for i in range(1, LINE):
            leg_line(ch, i).start()
        logits = logits + lax.dot_general(
            normed,
            router_ref[:, span],
            (((1,), (1,)), ((), ())),
            preferred_element_type=F32,
        )
    gates = jax.nn.sigmoid(logits)
    shares = route_scale * gates / jnp.sum(gates * named, axis=1, keepdims=True) * kept
    share_out[...] = jnp.zeros_like(share_out)
    share_out[:, :EXPERTS] = shares

    def share_copy(i):
        to = (me + i) % n
        return send(share_out, share_in.at[me], share_send.at[to], share_recv.at[me], to)

    def share_arrival(i):
        frm = (me + i) % n
        return send(share_out, share_in.at[frm], share_send.at[frm], share_recv.at[frm], frm)

    gate_acc[...] = jnp.zeros_like(gate_acc)
    up_acc[...] = jnp.zeros_like(up_acc)

    def hop_mid(ch):
        for i in range(1, LINE):
            leg_line_arrival(ch, (a + i) % LINE).wait_recv()
        loop(mids, lambda i: leg_mid(ch, i).start(), 1)

    def hop_core(ch):
        loop(mids, lambda i: leg_mid_arrival(ch, (b + i) % mids).wait_recv(), 1)
        leg_core(ch).start()

    def multiply(ch):
        leg_core_arrival(ch).wait_recv()

        def block(d):
            return gathered[ch, d % CORES, (d // CORES) % mids, d // fan].astype(F32)

        stack(acc32, block, toks)
        x = acc32[...].astype(BF16)
        wg_copy(ch).wait()
        gate_acc[...] += jnp.dot(x, wg[ch], preferred_element_type=F32)
        wu_copy(ch).wait()
        up_acc[...] += jnp.dot(x, wu[ch], preferred_element_type=F32)

    def gather_step(t):
        for delay, stage in enumerate((hop_mid, hop_core, multiply)):
            pl.when((t >= delay) & (t < CHUNKS + delay))(functools.partial(stage, t - delay))

    loop(n, lambda i: share_copy(i).start(), 1)
    loop(CHUNKS + 2, gather_step)

    share_in[me] = share_out[...]
    loop(n, lambda i: share_arrival(i).wait_recv(), 1)

    stack(share_all, lambda d: share_in[d], toks)
    mine = lax.broadcasted_iota(jnp.int32, share_all.shape, 1) == me // (n // EXPERTS)
    share = jnp.sum(jnp.where(mine, share_all[...], 0.0), axis=1, keepdims=True)
    gate = gate_acc[...]
    act = (gate * jax.nn.sigmoid(gate) * up_acc[...]).astype(BF16)

    def expert_part(ch):
        wd_copy(ch).wait()
        return jnp.dot(act, wd[ch], preferred_element_type=F32) * share

    def put_out(ch, acc):
        mixed = hid[ch] + acc
        for q in range(seqs):
            out_ref[q, :, cols(ch)] = mixed[q * steps : (q + 1) * steps].astype(BF16)

    reduce_scatter(1, expert_part, put_out)

    def drain_pairs(i):
        ctx_copy(i).wait_send()
        share_copy(i).wait_send()

    loop(n, drain_pairs, 1)

    def drain_gather(ch):
        for i in range(1, LINE):
            leg_line(ch, i).wait_send()
        loop(mids, lambda i: leg_mid(ch, i).wait_send(), 1)
        leg_core(ch).wait_send()

    loop(CHUNKS, drain_gather)


def body(
    cache_kv,
    new_kv,
    queries,
    lengths,
    resid,
    value_up,
    out_proj,
    norm_gain,
    router,
    expert_ids,
    slots,
    w_gate,
    w_up,
    w_down,
):
    n = lax.axis_size("ep")
    seqs, steps, heads, kv = queries.shape
    toks = seqs * steps
    width = resid.shape[-1]
    heads_per = max(1, value_up.shape[1] // VH)
    packets = (n, toks * heads_per, LAT)
    hidden_units = w_gate.shape[1]
    mids = n // (CORES * LINE)
    part_w = width // CHUNKS
    total = n * toks
    vmem = pl.BlockSpec(memory_space=pltpu.VMEM)
    hbm = pl.BlockSpec(memory_space=pl.ANY)
    landing = [
        pltpu.VMEM((CHUNKS, mids, LINE, toks, part_w), BF16),
        pltpu.VMEM((CHUNKS, mids, LINE, toks, part_w), BF16),
        pltpu.VMEM((CHUNKS, LINE, toks, part_w), BF16),
    ]
    dma = pltpu.SemaphoreType.DMA
    mixed = pl.pallas_call(
        functools.partial(layer_kernel, n),
        out_shape=jax.ShapeDtypeStruct(resid.shape, BF16),
        in_specs=[pl.BlockSpec(memory_space=pltpu.SMEM)] + [vmem] * 5 + [hbm] * 8,
        out_specs=vmem,
        scratch_shapes=[
            pltpu.VMEM(value_up.shape, BF16),
            pltpu.VMEM((CHUNKS, out_proj.shape[0], part_w), BF16),
            pltpu.VMEM((CHUNKS, part_w, hidden_units), BF16),
            pltpu.VMEM((CHUNKS, part_w, hidden_units), BF16),
            pltpu.VMEM((CHUNKS, hidden_units, part_w), BF16),
            pltpu.VMEM((seqs, kv, cache_kv.shape[1]), BF16),
            pltpu.VMEM((seqs, 128, kv), BF16),
            pltpu.VMEM((seqs, steps * heads, kv), BF16),
            pltpu.VMEM(resid.shape, BF16),
            pltpu.VMEM((seqs, steps * heads, LAT), F32),
            pltpu.VMEM(packets, BF16),
            pltpu.VMEM(packets, BF16),
            pltpu.VMEM((n * toks * heads_per if toks * heads_per % 16 else 8, LAT), F32),
            pltpu.VMEM((total, part_w), F32),
            pltpu.VMEM((total, hidden_units), F32),
            pltpu.VMEM((total, hidden_units), F32),
            pltpu.VMEM((CHUNKS, toks, part_w), F32),
            pltpu.VMEM((CHUNKS, CORES, mids, LINE, toks, part_w), BF16),
            pltpu.VMEM((CHUNKS, mids, LINE, toks, part_w), BF16),
            pltpu.VMEM((CHUNKS, LINE, toks, part_w), BF16),
            *landing,
            *landing,
            pltpu.VMEM((CHUNKS, CORES, mids, LINE, toks, part_w), BF16),
            pltpu.VMEM((toks, 128), F32),
            pltpu.VMEM((n, toks, 128), F32),
            pltpu.VMEM((total, 128), F32),
            dma((5, CHUNKS)),
            dma((2, seqs)),
            dma((n,)),
            dma((n,)),
            dma((n,)),
            dma((n,)),
            dma((3, 2, CHUNKS)),
            dma((3, CHUNKS, mids)),
            dma((3, CHUNKS, mids)),
            dma((3, CHUNKS, LINE)),
            dma((3, CHUNKS, LINE)),
        ],
        compiler_params=pltpu.CompilerParams(
            collective_id=0, has_side_effects=True, vmem_limit_bytes=67043328
        ),
    )(
        lengths,
        new_kv,
        norm_gain.reshape(1, width),
        router.T,
        expert_ids.reshape(toks, TOP),
        slots.reshape(toks, TOP),
        cache_kv.transpose(0, 2, 1),
        queries.reshape(seqs, steps * heads, kv),
        resid,
        value_up,
        out_proj,
        w_gate,
        w_up,
        w_down,
    )
    return mixed


def solution(mesh):
    return jax.shard_map(
        body,
        mesh=mesh,
        in_specs=(
            P(("rep", "ep"), None, None),
            P(("rep", "ep"), None, None),
            P(("rep", "ep"), None, None, None),
            P(("rep", "ep")),
            P(("rep", "ep"), None, None),
            P(None, "ep"),
            P("ep", None),
            P(),
            P(),
            P(("rep", "ep"), None, None),
            P(("rep", "ep"), None, None),
            P(None, "ep"),
            P(None, "ep"),
            P("ep", None),
        ),
        out_specs=P(("rep", "ep"), None, None),
        check_vma=False,
    )
```

profile of v0, /device:TPU:0, one launch (start us, length us, event | category | flops | bytes accessed | tf_op | source)
XLA Modules:
  0.0 75.7 jit_solution(13593303860467730593)
XLA Ops:
  0.0 1.3 %reshape.12.gain_ref = bf16[1,7168]{1,0:T(2,128)(2,1)} reshape(bf16[7168]{0:T(1024)(128)(2,1)} %param.21) | data formatting | bytes 28672 | tf_op jit(solution)/shard_map/reshape | solution.py:605
  1.3 72.9 %shard_map.136 = bf16[2,2,7168]{2,1,0:T(2,128)(2,1)} custom-call(s32[2]{0:T(128)} %len_ref.1, bf16[2,2,576]{2,1,0:T(2,128)(2,1)} %new_ref.1, bf16[1,7168]{1,0:T(2,128)(2,1)} %reshape.12.gain_ref, bf16[16,7168]{1,0:T(8,128)(2,1)} %bitcast.7, s32[4,8]{1,0:T(4,128)} %bitcast.8, s32[4,8]{1,0:T(4,128)} %bitcast.9, bf16[2,576,2048]{2,1,0:T(8,128)(2,1)} %bitcast.5, ...), custom_call_target="tpu_custom_call" | custom-call | tf_op jit(solution)/shard_map/pallas_call | solution.py:555
  74.3 1.5 %copy.16 = bf16[2,2,7168]{2,1,0:T(2,128)(2,1)} copy(bf16[2,2,7168]{2,1,0:T(2,128)(2,1)} %shard_map.136) | data formatting | bytes 114688
where the time goes:
time: 76 us; the launch traced here: 75.7 us
  Pallas kernels  72.9 us (96%)
  local copies, waits for them, and re-layouts  2.82 us (4%)
    pallas_call x1, Pallas kernels, body(): pl.pallas_call(functools.partial(layer_kernel, n), out_shape=jax.ShapeDty...  72.9 us

commit v1 on v0

v1 whole, which is shorter than its diff:
```python
import functools
import math

import jax
import jax.numpy as jnp
from jax import lax
from jax.experimental import pallas as pl
from jax.experimental.pallas import tpu as pltpu
from jax.sharding import PartitionSpec as P

H = 64
LAT = 512
VH = 128
EXPERTS = 16
TOP = 8
CAP = 2
QK = 192


route_scale = 2.827
norm_eps = 1e-06


F32 = jnp.float32
BF16 = jnp.bfloat16
CORES = 2
LINE = 4
CHUNKS = 7
LANES = 128
KEY_BLOCKS = 4

MERGED = (0, 1, 4, 7, 10, 12, 13)
SECOND = (0, 1, 4, 7)


def loop(count, step, start=0):
    lax.fori_loop(start, count, lambda i, carry: (step(i), carry)[1], 0)


def pipeline(stages, delays, extra=None):
    def step(t):
        for delay, stage in zip(delays, stages):
            pl.when((t >= delay) & (t < CHUNKS + delay))(functools.partial(stage, t - delay))
        if extra is not None:
            extra(t)

    loop(CHUNKS + delays[-1], step)


def layer_kernel(
    n,
    len_ref,
    new_hbm,
    gain_hbm,
    router_hbm,
    ids_hbm,
    slots_hbm,
    cache_hbm,
    query_hbm,
    resid_hbm,
    vu_hbm,
    op_hbm,
    wg_hbm,
    wu_hbm,
    wd_hbm,
    out_ref,
    vu,
    op,
    wg,
    wu,
    wd,
    keys,
    fresh,
    query,
    new_ref,
    gain_in,
    gain,
    router,
    ids_ref,
    slots_ref,
    resid,
    ctx32,
    ctx_ref,
    ctx_in,
    rows32,
    values,
    act,
    gate_acc,
    up_acc,
    hid,
    part,
    pair_sum,
    line_sum,
    in_core0,
    in_mid0,
    in_line0,
    in_core1,
    in_mid1,
    in_line1,
    block,
    gathered,
    share_out,
    share_in,
    share_all,
    w_sem,
    small_sem,
    key_sem,
    ctx_send,
    ctx_recv,
    share_sem,
    core_send,
    core_recv,
    mid_send,
    mid_recv,
    line_send,
    line_recv,
):
    me = lax.axis_index("ep")
    mids = n // (CORES * LINE)
    c = me % CORES
    b = (me // CORES) % mids
    a = me // (CORES * mids)
    seqs, steps, width = resid.shape
    toks = seqs * steps
    part_w = width // CHUNKS
    piece = ctx_ref.shape[2]
    heads_per = piece // steps
    value_cols = vu.shape[1]
    total = n * toks
    fan = CORES * mids
    group = LINE * toks

    def dev(aa, bb, cc):
        return (aa * mids + bb) * CORES + cc

    def slot(aa, bb, cc):
        return (cc * mids + bb) * LINE + aa

    my_slot = slot(a, b, c)
    far_first = (LINE - 1 - a, (a + 2) % LINE, a + 1 - 2 * (a % 2))

    def send(src, dst, s_sem, r_sem, target):
        return pltpu.make_async_remote_copy(
            src_ref=src,
            dst_ref=dst,
            send_sem=s_sem,
            recv_sem=r_sem,
            device_id={"ep": target},
            device_id_type=pl.DeviceIdType.MESH,
        )

    def settle(ref, sem):
        pltpu.make_async_copy(ref, ref, sem).wait()

    def cols(ch):
        return pl.ds(pl.multiple_of(ch * part_w, part_w), part_w)

    def op_copy(ch):
        return pltpu.make_async_copy(op_hbm.at[:, cols(ch)], op.at[ch], w_sem.at[0, ch])

    def wg_copy(ch):
        return pltpu.make_async_copy(wg_hbm.at[cols(ch), :], wg.at[ch], w_sem.at[1, ch])

    def wu_copy(ch):
        return pltpu.make_async_copy(wu_hbm.at[cols(ch), :], wu.at[ch], w_sem.at[2, ch])

    def wd_copy(ch):
        return pltpu.make_async_copy(wd_hbm.at[:, cols(ch)], wd.at[ch], w_sem.at[3, ch])

    cache_len = cache_hbm.shape[2]
    key_w = cache_len // KEY_BLOCKS

    def key_copy(q, j):
        span = pl.ds(j * key_w, key_w)
        return pltpu.make_async_copy(
            cache_hbm.at[q, :, span], keys.at[q, :, span], key_sem.at[q, j]
        )

    def query_copy(q):
        return pltpu.make_async_copy(query_hbm.at[q], query.at[q], key_sem.at[q, KEY_BLOCKS])

    new_copy = pltpu.make_async_copy(new_hbm, new_ref, small_sem.at[0])
    vu_copy = pltpu.make_async_copy(vu_hbm, vu, small_sem.at[1])
    resid_copy = pltpu.make_async_copy(resid_hbm, resid, small_sem.at[2])
    gain_copy = pltpu.make_async_copy(gain_hbm, gain_in, small_sem.at[3])
    router_copy = pltpu.make_async_copy(router_hbm, router, small_sem.at[4])
    ids_copy = pltpu.make_async_copy(ids_hbm, ids_ref, small_sem.at[5])
    slots_copy = pltpu.make_async_copy(slots_hbm, slots_ref, small_sem.at[6])

    new_copy.start()
    for q in range(seqs):
        query_copy(q).start()
        for j in range(KEY_BLOCKS):
            key_copy(q, j).start()
    for small in (vu_copy, resid_copy, gain_copy, router_copy, ids_copy, slots_copy):
        small.start()

    barrier = pltpu.get_barrier_semaphore()

    def greet(i):
        pl.semaphore_signal(
            barrier,
            inc=1,
            device_id={"ep": (me + i) % n},
            device_id_type=pl.DeviceIdType.MESH,
        )

    loop(n, greet, 1)
    loop(CHUNKS, lambda ch: op_copy(ch).start())

    def start_ffn(ch):
        wg_copy(ch).start()
        wu_copy(ch).start()

    loop(CHUNKS, start_ffn)
    loop(CHUNKS, lambda ch: wd_copy(ch).start())

    rows_q, span_new = query.shape[1], fresh.shape[1]
    heads = rows_q // steps
    score_scale = math.log2(math.e) / math.sqrt(QK)
    fresh[...] = jnp.zeros_like(fresh)
    gate_acc[...] = jnp.zeros_like(gate_acc)
    up_acc[...] = jnp.zeros_like(up_acc)
    share_out[...] = jnp.zeros_like(share_out)
    newer = lax.broadcasted_iota(jnp.int32, (rows_q, span_new), 1) <= (
        lax.broadcasted_iota(jnp.int32, (rows_q, span_new), 0) // heads
    )
    place = lax.broadcasted_iota(jnp.int32, (rows_q, key_w), 1)
    across = (((1,), (1,)), ((), ()))

    def attend(q):
        query_copy(q).wait()
        new = lax.dot_general(query[q], fresh[q], across, preferred_element_type=F32)
        new = jnp.where(newer, new, -jnp.inf)
        peak = jnp.max(new, axis=-1, keepdims=True)
        for j in range(KEY_BLOCKS):
            key_copy(q, j).wait()
        old = []
        for j in range(KEY_BLOCKS):
            score = jnp.dot(
                query[q], keys[q, :, j * key_w : (j + 1) * key_w], preferred_element_type=F32
            )
            score = jnp.where(place < len_ref[q] - j * key_w, score, -jnp.inf)
            peak = jnp.maximum(peak, jnp.max(score, axis=-1, keepdims=True))
            old.append(score)
        new = jnp.exp2((new - peak) * score_scale)
        weight = jnp.sum(new, axis=-1, keepdims=True)
        context = jnp.dot(new.astype(BF16), fresh[q, :, :LAT], preferred_element_type=F32)
        for j in range(KEY_BLOCKS):
            prob = jnp.exp2((old[j] - peak) * score_scale)
            weight = weight + jnp.sum(prob, axis=-1, keepdims=True)
            context = context + lax.dot_general(
                prob.astype(BF16),
                keys[q, :LAT, j * key_w : (j + 1) * key_w],
                across,
                preferred_element_type=F32,
            )
        ctx32[q] = context * (1.0 / weight)
        for j in range(n):
            first = (j * value_cols) // VH
            rows = [
                ctx32[q, t * heads + first : t * heads + first + heads_per, :]
                for t in range(steps)
            ]
            ctx_ref[q, j] = jnp.concatenate(rows, axis=0).astype(BF16)

    def ctx_start(q):
        def one(to):
            send(
                ctx_ref.at[q, to],
                ctx_in.at[q, my_slot],
                ctx_send.at[0],
                ctx_recv.at[q],
                to,
            ).start()

        for aa in far_first:
            loop(fan, lambda i: one(aa * fan + (me + i) % fan))
        loop(fan, lambda i: one(a * fan + (me + i) % fan), 1)

    new_copy.wait()
    for q in range(seqs):
        fresh[q, :steps, :] = new_ref[q]
    with jax.named_scope("attn0"):
        attend(0)
    with jax.named_scope("barrier"):
        pl.semaphore_wait(barrier, n - 1)
    with jax.named_scope("send0"):
        ctx_start(0)
    for q in range(1, seqs):
        with jax.named_scope("attn1"):
            attend(q)
        with jax.named_scope("send1"):
            ctx_start(q)

    with jax.named_scope("prep"):
        ids_copy.wait()
        slots_copy.wait()
        lane = lax.broadcasted_iota(jnp.int32, (toks, EXPERTS), 1)
        named = jnp.zeros((toks, EXPERTS), F32)
        kept = jnp.zeros((toks, EXPERTS), F32)
        for k in range(TOP):
            hit = jnp.where(ids_ref[:, k : k + 1] == lane, 1.0, 0.0)
            named = named + hit
            kept = kept + jnp.where(slots_ref[:, k : k + 1] < CAP, hit, 0.0)
        resid_copy.wait()
        gain_copy.wait()
        per = part_w // LANES
        for ch in range(CHUNKS):
            rows = [resid[q, :, ch * part_w : (ch + 1) * part_w].astype(F32) for q in range(seqs)]
            hid[ch] = jnp.concatenate(rows, axis=0)
            wide = gain_in[ch * per : (ch + 1) * per, :].astype(F32)
            gain[ch] = jnp.concatenate([wide[k : k + 1] for k in range(per)], axis=1)
        vu_copy.wait()

    def fold_values(q):
        settle(ctx_in.at[q, pl.ds(0, n - 1)], ctx_recv.at[q])
        bunch = 8 // piece

        def put(g):
            tile = [ctx_in[q, g * bunch + h].astype(F32) for h in range(bunch)]
            rows32[pl.ds(pl.multiple_of(g * 8, 8), 8), :] = (
                jnp.concatenate(tile, axis=0) if bunch > 1 else tile[0]
            )

        loop(n // bunch, put)
        mixed = jnp.dot(rows32[...].astype(BF16), vu[...], preferred_element_type=F32)
        shape = (n * piece, value_cols)
        row_head = lax.broadcasted_iota(jnp.int32, shape, 0) % heads_per
        col_head = lax.broadcasted_iota(jnp.int32, shape, 1) // (value_cols // heads_per)
        mixed = jnp.where(row_head == col_head, mixed, 0.0).astype(BF16)
        shape = (total, n * piece)
        came = lax.broadcasted_iota(jnp.int32, shape, 1)
        row_tok = (came // piece) * toks + q * steps + (came % piece) // heads_per
        fold = jnp.where(row_tok == lax.broadcasted_iota(jnp.int32, shape, 0), 1.0, 0.0)
        return jnp.dot(fold.astype(BF16), mixed, preferred_element_type=F32)

    for q in range(seqs):
        ctx_in[q, my_slot] = ctx_ref[q, me]
    folded = None
    for q in range(seqs):
        with jax.named_scope("values"):
            term = fold_values(q)
            folded = term if folded is None else folded + term
    values[...] = folded.astype(BF16)

    def reduce_scatter(which, product, finish):
        in_core, in_mid, in_line = (
            (in_core0, in_mid0, in_line0) if which == 0 else (in_core1, in_mid1, in_line1)
        )

        def core_copy(ch):
            return send(
                part.at[ch, 1 - c],
                in_core.at[ch],
                core_send.at[which],
                core_recv.at[which, ch],
                dev(a, b, 1 - c),
            )

        def mid_copy(ch, bb):
            return send(
                pair_sum.at[ch, bb],
                in_mid.at[ch, b],
                mid_send.at[which],
                mid_recv.at[which, ch],
                dev(a, bb, c),
            )

        def line_copy(ch, aa):
            return send(
                line_sum.at[ch, aa],
                in_line.at[ch, a],
                line_send.at[which],
                line_recv.at[which, ch],
                dev(aa, b, c),
            )

        def stage1(ch):
            whole = product(ch).astype(BF16).reshape(CORES, mids, group, part_w)
            part[ch] = whole
            core_copy(ch).start()

        def stage2(ch):
            settle(in_core.at[ch], core_recv.at[which, ch])

            def pair(bb):
                pair_sum[ch, bb] = (
                    part[ch, c, bb].astype(F32) + in_core[ch, bb].astype(F32)
                ).astype(BF16)

            def pair_send(i):
                bb = (b + i) % mids
                pair(bb)
                mid_copy(ch, bb).start()

            loop(mids, pair_send, 1)
            pair(b)

        def stage3(ch):
            settle(in_mid.at[ch, pl.ds(0, mids - 1)], mid_recv.at[which, ch])
            acc = pair_sum[ch, b].astype(F32)
            acc = lax.fori_loop(
                1, mids, lambda i, t: t + in_mid[ch, (b + i) % mids].astype(F32), acc
            )
            for aa in range(LINE):
                line_sum[ch, aa] = acc[aa * toks : (aa + 1) * toks].astype(BF16)
            for aa in far_first:
                line_copy(ch, aa).start()

        def stage4(ch):
            settle(in_line.at[ch, pl.ds(0, LINE - 1)], line_recv.at[which, ch])
            acc = line_sum[ch, a].astype(F32)
            for aa in far_first:
                acc = acc + in_line[ch, aa].astype(F32)
            finish(ch, acc)

        def drain():
            settle(in_core, core_send.at[which])
            settle(in_mid.at[:, pl.ds(0, mids - 1)], mid_send.at[which])
            settle(in_line.at[:, pl.ds(0, LINE - 1)], line_send.at[which])

        return (stage1, stage2, stage3, stage4), drain

    def attended_part(ch):
        op_copy(ch).wait()
        return jnp.dot(values[...], op[ch], preferred_element_type=F32)

    def spread_hidden(ch, acc):
        hidden = hid[ch] + acc
        hid[ch] = hidden
        block[ch, a] = (hidden * gain[ch]).astype(BF16)
        for aa in far_first:
            send(
                block.at[ch, a],
                block.at[ch, a],
                line_send.at[2],
                line_recv.at[2, ch],
                dev(aa, b, c),
            ).start()

    def hop_mid(ch):
        settle(block.at[ch, pl.ds(0, LINE - 1)], line_recv.at[2, ch])
        rows = [block[ch, aa].astype(F32) for aa in range(LINE)]
        gathered[ch, c, b] = jnp.concatenate(rows, axis=0).astype(BF16)
        ours = gathered.at[ch, c, b]

        def forward(i):
            send(
                ours, ours, mid_send.at[2], mid_recv.at[2, ch], dev(a, (b + i) % mids, c)
            ).start()

        loop(mids, forward, 1)

    def hop_core(ch):
        settle(gathered.at[ch, c, pl.ds(0, mids - 1)], mid_recv.at[2, ch])
        ours = gathered.at[ch, c]
        send(ours, ours, core_send.at[2], core_recv.at[2, ch], dev(a, b, 1 - c)).start()

    def multiply(ch):
        settle(gathered.at[ch, 1 - c], core_recv.at[2, ch])
        rows = gathered[ch].reshape(total, part_w)
        wg_copy(ch).wait()
        gate_acc[...] += jnp.dot(rows, wg[ch], preferred_element_type=F32)
        wu_copy(ch).wait()
        up_acc[...] += jnp.dot(rows, wu[ch], preferred_element_type=F32)

    def route():
        router_copy.wait()
        square = jnp.zeros((toks, part_w), F32)
        logits = jnp.zeros((toks, EXPERTS), F32)
        for ch in range(CHUNKS):
            hidden = hid[ch]
            square = square + hidden * hidden
            logits = logits + lax.dot_general(
                block[ch, a],
                router[:, ch * part_w : (ch + 1) * part_w],
                across,
                preferred_element_type=F32,
            )
        scale = lax.rsqrt(jnp.sum(square, axis=-1, keepdims=True) / width + norm_eps)
        gates = jax.nn.sigmoid(logits * scale)
        shares = route_scale * gates / jnp.sum(gates * named, axis=1, keepdims=True) * kept
        share_out[:, :EXPERTS] = shares
        share_out[:, EXPERTS : EXPERTS + 1] = scale

        def share_start(i):
            send(
                share_out, share_in.at[my_slot], share_sem.at[0], share_sem.at[1], (me + i) % n
            ).start()

        loop(n, share_start, 1)
        share_in[my_slot] = share_out[...]

    first_stages, first_drain = reduce_scatter(0, attended_part, spread_hidden)

    def scoped(f):
        def g(*args):
            with jax.named_scope(f.__name__):
                f(*args)

        return g

    with jax.named_scope("merged"):
        pipeline(
            [scoped(f) for f in first_stages + (hop_mid, hop_core, multiply)],
            MERGED,
            lambda t: pl.when(t == CHUNKS + MERGED[3] - 1)(scoped(route)),
        )

    with jax.named_scope("act"):
        settle(share_in.at[pl.ds(0, n - 1)], share_sem.at[1])
        bunch = 8 // toks

        def put_share(g):
            tile = [share_in[g * bunch + h] for h in range(bunch)]
            share_all[pl.ds(pl.multiple_of(g * 8, 8), 8), :] = (
                jnp.concatenate(tile, axis=0) if bunch > 1 else tile[0]
            )

        loop(n // bunch, put_share)
        sent = share_all[...]
        mine = lax.broadcasted_iota(jnp.int32, share_all.shape, 1) == me // (n // EXPERTS)
        share = jnp.sum(jnp.where(mine, sent, 0.0), axis=1, keepdims=True)
        scale = sent[:, EXPERTS : EXPERTS + 1]
        gate = gate_acc[...] * scale
        act[...] = (gate * jax.nn.sigmoid(gate) * up_acc[...] * (scale * share)).astype(BF16)
        first_drain()

    def expert_part(ch):
        wd_copy(ch).wait()
        return jnp.dot(act[...], wd[ch], preferred_element_type=F32)

    def put_out(ch, acc):
        mixed = hid[ch] + acc
        for q in range(seqs):
            out_ref[q, :, cols(ch)] = mixed[q * steps : (q + 1) * steps].astype(BF16)

    second_stages, second_drain = reduce_scatter(1, expert_part, put_out)
    with jax.named_scope("rs2"):
        pipeline([scoped(f) for f in second_stages], SECOND)

    with jax.named_scope("drain"):
        second_drain()
        settle(ctx_in.at[:, pl.ds(0, n - 1)], ctx_send.at[0])
        settle(share_in.at[pl.ds(0, n - 1)], share_sem.at[0])
        settle(block.at[:, pl.ds(0, LINE - 1)], line_send.at[2])
        settle(gathered.at[:, 0, pl.ds(0, mids - 1)], mid_send.at[2])
        settle(gathered.at[:, 0], core_send.at[2])


def body(
    cache_kv,
    new_kv,
    queries,
    lengths,
    resid,
    value_up,
    out_proj,
    norm_gain,
    router,
    expert_ids,
    slots,
    w_gate,
    w_up,
    w_down,
):
    n = lax.axis_size("ep")
    seqs, steps, heads, kv = queries.shape
    toks = seqs * steps
    width = resid.shape[-1]
    heads_per = max(1, value_up.shape[1] // VH)
    packets = (seqs, n, steps * heads_per, LAT)
    hidden_units = w_gate.shape[1]
    mids = n // (CORES * LINE)
    part_w = width // CHUNKS
    total = n * toks
    group = LINE * toks
    vmem = pl.BlockSpec(memory_space=pltpu.VMEM)
    hbm = pl.BlockSpec(memory_space=pl.ANY)
    landing = [
        pltpu.VMEM((CHUNKS, mids, group, part_w), BF16),
        pltpu.VMEM((CHUNKS, mids, group, part_w), BF16),
        pltpu.VMEM((CHUNKS, LINE, toks, part_w), BF16),
    ]
    dma = pltpu.SemaphoreType.DMA
    mixed = pl.pallas_call(
        functools.partial(layer_kernel, n),
        out_shape=jax.ShapeDtypeStruct(resid.shape, BF16),
        in_specs=[pl.BlockSpec(memory_space=pltpu.SMEM)] + [hbm] * 13,
        out_specs=vmem,
        scratch_shapes=[
            pltpu.VMEM(value_up.shape, BF16),
            pltpu.VMEM((CHUNKS, out_proj.shape[0], part_w), BF16),
            pltpu.VMEM((CHUNKS, part_w, hidden_units), BF16),
            pltpu.VMEM((CHUNKS, part_w, hidden_units), BF16),
            pltpu.VMEM((CHUNKS, hidden_units, part_w), BF16),
            pltpu.VMEM((seqs, kv, cache_kv.shape[1]), BF16),
            pltpu.VMEM((seqs, LANES, kv), BF16),
            pltpu.VMEM((seqs, steps * heads, kv), BF16),
            pltpu.VMEM(new_kv.shape, BF16),
            pltpu.VMEM((width // LANES, LANES), BF16),
            pltpu.VMEM((CHUNKS, 1, part_w), F32),
            pltpu.VMEM((router.shape[1], width), BF16),
            pltpu.VMEM((toks, TOP), jnp.int32),
            pltpu.VMEM((toks, TOP), jnp.int32),
            pltpu.VMEM(resid.shape, BF16),
            pltpu.VMEM((seqs, steps * heads, LAT), F32),
            pltpu.VMEM(packets, BF16),
            pltpu.VMEM(packets, BF16),
            pltpu.VMEM((n * steps * heads_per, LAT), F32),
            pltpu.VMEM((total, value_up.shape[1]), BF16),
            pltpu.VMEM((total, hidden_units), BF16),
            pltpu.VMEM((total, hidden_units), F32),
            pltpu.VMEM((total, hidden_units), F32),
            pltpu.VMEM((CHUNKS, toks, part_w), F32),
            pltpu.VMEM((CHUNKS, CORES, mids, group, part_w), BF16),
            pltpu.VMEM((CHUNKS, mids, group, part_w), BF16),
            pltpu.VMEM((CHUNKS, LINE, toks, part_w), BF16),
            *landing,
            *landing,
            pltpu.VMEM((CHUNKS, LINE, toks, part_w), BF16),
            pltpu.VMEM((CHUNKS, CORES, mids, group, part_w), BF16),
            pltpu.VMEM((toks, LANES), F32),
            pltpu.VMEM((n, toks, LANES), F32),
            pltpu.VMEM((total, LANES), F32),
            dma((4, CHUNKS)),
            dma((7,)),
            dma((seqs, KEY_BLOCKS + 1)),
            dma((1,)),
            dma((seqs,)),
            dma((2,)),
            dma((3,)),
            dma((3, CHUNKS)),
            dma((3,)),
            dma((3, CHUNKS)),
            dma((3,)),
            dma((3, CHUNKS)),
        ],
        compiler_params=pltpu.CompilerParams(
            collective_id=0, has_side_effects=True, vmem_limit_bytes=67043328
        ),
    )(
        lengths,
        new_kv,
        norm_gain.reshape(width // LANES, LANES),
        router.T,
        expert_ids.reshape(toks, TOP),
        slots.reshape(toks, TOP),
        cache_kv.transpose(0, 2, 1),
        queries.reshape(seqs, steps * heads, kv),
        resid,
        value_up,
        out_proj,
        w_gate,
        w_up,
        w_down,
    )
    return mixed


def solution(mesh):
    return jax.shard_map(
        body,
        mesh=mesh,
        in_specs=(
            P(("rep", "ep"), None, None),
            P(("rep", "ep"), None, None),
            P(("rep", "ep"), None, None, None),
            P(("rep", "ep")),
            P(("rep", "ep"), None, None),
            P(None, "ep"),
            P("ep", None),
            P(),
            P(),
            P(("rep", "ep"), None, None),
            P(("rep", "ep"), None, None),
            P(None, "ep"),
            P(None, "ep"),
            P("ep", None),
        ),
        out_specs=P(("rep", "ep"), None, None),
        check_vma=False,
    )
```

time: 76 us -> 57.1 us (0.75)
  Pallas kernels: 72.9 us -> 55.5 us
  local copies, waits for them, and re-layouts: 2.82 us -> 1.48 us
    pallas_call x1, Pallas kernels: 72.9 us -> 55.5 us  [body(): pl.pallas_call(functools.partial(layer_kernel, n), out_shape=jax.ShapeDty...]
    reshape x1 -> x0, local copies, waits for them, and re-layouts: 1.34 us -> none  [body(): norm_gain.reshape(1, width)]
where the time goes in v1:
time: 57.1 us; the launch traced here: 57 us
  Pallas kernels  55.5 us (97%)
  local copies, waits for them, and re-layouts  1.48 us (3%)
    pallas_call x1, Pallas kernels, body(): pl.pallas_call(functools.partial(layer_kernel, n), out_shape=jax.ShapeDty...  55.5 us
    unnamed x1, local copies, waits for them, and re-layouts  1.48 us

profile of v1, /device:TPU:0, one launch (start us, length us, event | category | flops | bytes accessed | tf_op | source)
XLA Modules:
  0.0 57.0 jit_solution(2916600920423543085)
XLA Ops:
  0.0 55.5 %shard_map.136 = bf16[2,2,7168]{2,1,0:T(2,128)(2,1)} custom-call(s32[2]{0:T(128)} %len_ref.1, bf16[2,2,576]{2,1,0:T(2,128)(2,1)} %new_hbm.1, bf16[56,128]{1,0:T(8,128)(2,1)} %bitcast.9, bf16[16,7168]{1,0:T(8,128)(2,1)} %bitcast.8, s32[4,8]{1,0:T(4,128)} %bitcast.10, s32[4,8]{1,0:T(4,128)} %bitcast.11, bf16[2,576,2048]{2,1,0:T(8,128)(2,1)} %bitcast.6, ...), custom_call_target="tpu_custom_call" | custom-call | tf_op jit(solution)/shard_map/pallas_call | solution.py:587
  55.5 1.5 %copy.16 = bf16[2,2,7168]{2,1,0:T(2,128)(2,1)} copy(bf16[2,2,7168]{2,1,0:T(2,128)(2,1)} %shard_map.136) | data formatting | bytes 114688

commit v2 on v1

--- a/solution.py
+++ b/solution.py
@@ -27,24 +27,54 @@
 LINE = 4
 CHUNKS = 7
 LANES = 128
-KEY_BLOCKS = 4
-
-MERGED = (0, 1, 4, 7, 10, 12, 13)
-SECOND = (0, 1, 4, 7)
+WEIGHT_CUTS = 4
+KEY_BLOCKS = 2
+
+LATENCY = {"core": 1.0, "mid": 2.3, "line": 3.0}
+OCCUPY = {"core": 0.7, "mid": 4.9, "line": 4.9}
 
 
 def loop(count, step, start=0):
     lax.fori_loop(start, count, lambda i, carry: (step(i), carry)[1], 0)
 
 
-def pipeline(stages, delays, extra=None):
-    def step(t):
-        for delay, stage in zip(delays, stages):
-            pl.when((t >= delay) & (t < CHUNKS + delay))(functools.partial(stage, t - delay))
-        if extra is not None:
-            extra(t)
-
-    loop(CHUNKS + delays[-1], step)
+def plan(work, hops):
+    last = len(work) - 1
+    ready = {(0, ch): 0.0 for ch in range(CHUNKS)}
+    upcoming = [0] * len(work)
+    free = dict.fromkeys(LATENCY, 0.0)
+    now, order = 0.0, []
+    while len(order) < CHUNKS * len(work):
+        open_events = [
+            (ready[stage, ch], stage, ch)
+            for stage, ch in enumerate(upcoming)
+            if (stage, ch) in ready
+        ]
+        runnable = [event for event in open_events if event[0] <= now + 1e-9]
+        if runnable:
+            late = (0, last) if last > 3 else (0,)
+            _, stage, ch = min(runnable, key=lambda e: (e[1] in late[1:], e[1] in late, -e[1]))
+        else:
+            now, stage, ch = min(open_events)
+        now += work[stage]
+        order.append((stage, ch))
+        upcoming[stage] += 1
+        if stage < last:
+            hop = hops[stage]
+            free[hop] = max(free[hop], now) + OCCUPY[hop] / CHUNKS
+            ready[stage + 1, ch] = free[hop] + LATENCY[hop]
+    return order
+
+
+def share_of(times):
+    return [0.05 + time / CHUNKS for time in times]
+
+
+MERGED = plan(
+    share_of((2.0, 0.35, 0.35, 0.5, 0.35, 0.0, 5.7)),
+    ("core", "mid", "line", "line", "mid", "core"),
+)
+SECOND = plan(share_of((3.1, 0.35, 0.35, 0.5)), ("core", "mid", "line"))
 
 
 def layer_kernel(
@@ -63,11 +93,10 @@
     wg_hbm,
     wu_hbm,
     wd_hbm,
-    out_ref,
+    out_hbm,
     vu,
     op,
-    wg,
-    wu,
+    wgu,
     wd,
     keys,
     fresh,
@@ -85,23 +114,21 @@
     rows32,
     values,
     act,
-    gate_acc,
-    up_acc,
+    ffn_acc,
     hid,
     part,
     pair_sum,
     line_sum,
-    in_core0,
-    in_mid0,
-    in_line0,
-    in_core1,
-    in_mid1,
-    in_line1,
+    in_core,
+    in_mid,
+    in_line,
     block,
     gathered,
     share_out,
     share_in,
     share_all,
+    out_ref,
+    out_sem,
     w_sem,
     small_sem,
     key_sem,
@@ -126,6 +153,7 @@
     piece = ctx_ref.shape[2]
     heads_per = piece // steps
     value_cols = vu.shape[1]
+    hidden_units = wd.shape[0]
     total = n * toks
     fan = CORES * mids
     group = LINE * toks
@@ -153,19 +181,19 @@
         pltpu.make_async_copy(ref, ref, sem).wait()
 
     def cols(ch):
-        return pl.ds(pl.multiple_of(ch * part_w, part_w), part_w)
-
-    def op_copy(ch):
-        return pltpu.make_async_copy(op_hbm.at[:, cols(ch)], op.at[ch], w_sem.at[0, ch])
-
-    def wg_copy(ch):
-        return pltpu.make_async_copy(wg_hbm.at[cols(ch), :], wg.at[ch], w_sem.at[1, ch])
-
-    def wu_copy(ch):
-        return pltpu.make_async_copy(wu_hbm.at[cols(ch), :], wu.at[ch], w_sem.at[2, ch])
-
-    def wd_copy(ch):
-        return pltpu.make_async_copy(wd_hbm.at[:, cols(ch)], wd.at[ch], w_sem.at[3, ch])
+        return pl.ds(ch * part_w, part_w)
+
+    def weight_start(hbm, vmem, sem):
+        tall = hbm.shape[0] // WEIGHT_CUTS
+
+        def one(k):
+            span = pl.ds(pl.multiple_of(k * tall, tall), tall)
+            pltpu.make_async_copy(hbm.at[span], vmem.at[span], sem).start()
+
+        loop(WEIGHT_CUTS, one)
+
+    w_gate = wgu.at[:, pl.ds(0, hidden_units)]
+    w_up = wgu.at[:, pl.ds(hidden_units, hidden_units)]
 
     cache_len = cache_hbm.shape[2]
     key_w = cache_len // KEY_BLOCKS
@@ -187,13 +215,13 @@
     ids_copy = pltpu.make_async_copy(ids_hbm, ids_ref, small_sem.at[5])
     slots_copy = pltpu.make_async_copy(slots_hbm, slots_ref, small_sem.at[6])
 
-    new_copy.start()
-    for q in range(seqs):
+    def keys_start(q):
         query_copy(q).start()
         for j in range(KEY_BLOCKS):
             key_copy(q, j).start()
-    for small in (vu_copy, resid_copy, gain_copy, router_copy, ids_copy, slots_copy):
-        small.start()
+
+    keys_start(0)
+    new_copy.start()
 
     barrier = pltpu.get_barrier_semaphore()
 
@@ -206,22 +234,22 @@
         )
 
     loop(n, greet, 1)
-    loop(CHUNKS, lambda ch: op_copy(ch).start())
-
-    def start_ffn(ch):
-        wg_copy(ch).start()
-        wu_copy(ch).start()
-
-    loop(CHUNKS, start_ffn)
-    loop(CHUNKS, lambda ch: wd_copy(ch).start())
+
+    for q in range(1, seqs):
+        keys_start(q)
+    for small in (vu_copy, resid_copy, gain_copy, router_copy, ids_copy, slots_copy):
+        small.start()
+
+    def start_weights():
+        weight_start(op_hbm, op, w_sem.at[0])
+        weight_start(wg_hbm, w_gate, w_sem.at[1])
+        weight_start(wu_hbm, w_up, w_sem.at[2])
+        weight_start(wd_hbm, wd, w_sem.at[3])
 
     rows_q, span_new = query.shape[1], fresh.shape[1]
     heads = rows_q // steps
     score_scale = math.log2(math.e) / math.sqrt(QK)
     fresh[...] = jnp.zeros_like(fresh)
-    gate_acc[...] = jnp.zeros_like(gate_acc)
-    up_acc[...] = jnp.zeros_like(up_acc)
-    share_out[...] = jnp.zeros_like(share_out)
     newer = lax.broadcasted_iota(jnp.int32, (rows_q, span_new), 1) <= (
         lax.broadcasted_iota(jnp.int32, (rows_q, span_new), 0) // heads
     )
@@ -229,12 +257,20 @@
     across = (((1,), (1,)), ((), ()))
 
     def attend(q):
+        def keys_here():
+            for j in range(KEY_BLOCKS):
+                key_copy(q, j).wait()
+            if q == seqs - 1:
+                start_weights()
+
         query_copy(q).wait()
+        if q > 0:
+            keys_here()
         new = lax.dot_general(query[q], fresh[q], across, preferred_element_type=F32)
         new = jnp.where(newer, new, -jnp.inf)
         peak = jnp.max(new, axis=-1, keepdims=True)
-        for j in range(KEY_BLOCKS):
-            key_copy(q, j).wait()
+        if q == 0:
+            keys_here()
         old = []
         for j in range(KEY_BLOCKS):
             score = jnp.dot(
@@ -278,7 +314,8 @@
             loop(fan, lambda i: one(aa * fan + (me + i) % fan))
         loop(fan, lambda i: one(a * fan + (me + i) % fan), 1)
 
-    new_copy.wait()
+    with jax.named_scope('new_wait'):
+        new_copy.wait()
     for q in range(seqs):
         fresh[q, :steps, :] = new_ref[q]
     with jax.named_scope("attn0"):
@@ -294,6 +331,7 @@
             ctx_start(q)
 
     with jax.named_scope("prep"):
+        share_out[...] = jnp.zeros_like(share_out)
         ids_copy.wait()
         slots_copy.wait()
         lane = lax.broadcasted_iota(jnp.int32, (toks, EXPERTS), 1)
@@ -344,17 +382,14 @@
             folded = term if folded is None else folded + term
     values[...] = folded.astype(BF16)
 
-    def reduce_scatter(which, product, finish):
-        in_core, in_mid, in_line = (
-            (in_core0, in_mid0, in_line0) if which == 0 else (in_core1, in_mid1, in_line1)
-        )
+    def reduce_scatter(product, finish):
 
         def core_copy(ch):
             return send(
                 part.at[ch, 1 - c],
                 in_core.at[ch],
-                core_send.at[which],
-                core_recv.at[which, ch],
+                core_send.at[0],
+                core_recv.at[0, ch],
                 dev(a, b, 1 - c),
             )
 
@@ -362,8 +397,8 @@
             return send(
                 pair_sum.at[ch, bb],
                 in_mid.at[ch, b],
-                mid_send.at[which],
-                mid_recv.at[which, ch],
+                mid_send.at[0],
+                mid_recv.at[0, ch],
                 dev(a, bb, c),
             )
 
@@ -371,8 +406,8 @@
             return send(
                 line_sum.at[ch, aa],
                 in_line.at[ch, a],
-                line_send.at[which],
-                line_recv.at[which, ch],
+                line_send.at[0],
+                line_recv.at[0, ch],
                 dev(aa, b, c),
             )
 
@@ -382,7 +417,7 @@
             core_copy(ch).start()
 
         def stage2(ch):
-            settle(in_core.at[ch], core_recv.at[which, ch])
+            settle(in_core.at[ch], core_recv.at[0, ch])
 
             def pair(bb):
                 pair_sum[ch, bb] = (
@@ -398,7 +433,7 @@
             pair(b)
 
         def stage3(ch):
-            settle(in_mid.at[ch, pl.ds(0, mids - 1)], mid_recv.at[which, ch])
+            settle(in_mid.at[ch, pl.ds(0, mids - 1)], mid_recv.at[0, ch])
             acc = pair_sum[ch, b].astype(F32)
             acc = lax.fori_loop(
                 1, mids, lambda i, t: t + in_mid[ch, (b + i) % mids].astype(F32), acc
@@ -409,22 +444,23 @@
                 line_copy(ch, aa).start()
 
         def stage4(ch):
-            settle(in_line.at[ch, pl.ds(0, LINE - 1)], line_recv.at[which, ch])
+            settle(in_line.at[ch, pl.ds(0, LINE - 1)], line_recv.at[0, ch])
             acc = line_sum[ch, a].astype(F32)
             for aa in far_first:
                 acc = acc + in_line[ch, aa].astype(F32)
             finish(ch, acc)
 
         def drain():
-            settle(in_core, core_send.at[which])
-            settle(in_mid.at[:, pl.ds(0, mids - 1)], mid_send.at[which])
-            settle(in_line.at[:, pl.ds(0, LINE - 1)], line_send.at[which])
+            settle(in_core, core_send.at[0])
+            settle(in_mid.at[:, pl.ds(0, mids - 1)], mid_send.at[0])
+            settle(in_line.at[:, pl.ds(0, LINE - 1)], line_send.at[0])
 
         return (stage1, stage2, stage3, stage4), drain
 
     def attended_part(ch):
-        op_copy(ch).wait()
-        return jnp.dot(values[...], op[ch], preferred_element_type=F32)
+        if ch == 0:
+            settle(op, w_sem.at[0])
+        return jnp.dot(values[...], op[:, cols(ch)], preferred_element_type=F32)
 
     def spread_hidden(ch, acc):
         hidden = hid[ch] + acc
@@ -434,36 +470,39 @@
             send(
                 block.at[ch, a],
                 block.at[ch, a],
-                line_send.at[2],
-                line_recv.at[2, ch],
+                line_send.at[1],
+                line_recv.at[1, ch],
                 dev(aa, b, c),
             ).start()
 
     def hop_mid(ch):
-        settle(block.at[ch, pl.ds(0, LINE - 1)], line_recv.at[2, ch])
+        settle(block.at[ch, pl.ds(0, LINE - 1)], line_recv.at[1, ch])
         rows = [block[ch, aa].astype(F32) for aa in range(LINE)]
         gathered[ch, c, b] = jnp.concatenate(rows, axis=0).astype(BF16)
         ours = gathered.at[ch, c, b]
 
         def forward(i):
             send(
-                ours, ours, mid_send.at[2], mid_recv.at[2, ch], dev(a, (b + i) % mids, c)
+                ours, ours, mid_send.at[1], mid_recv.at[1, ch], dev(a, (b + i) % mids, c)
             ).start()
 
         loop(mids, forward, 1)
 
     def hop_core(ch):
-        settle(gathered.at[ch, c, pl.ds(0, mids - 1)], mid_recv.at[2, ch])
+        settle(gathered.at[ch, c, pl.ds(0, mids - 1)], mid_recv.at[1, ch])
         ours = gathered.at[ch, c]
-        send(ours, ours, core_send.at[2], core_recv.at[2, ch], dev(a, b, 1 - c)).start()
+        send(ours, ours, core_send.at[1], core_recv.at[1, ch], dev(a, b, 1 - c)).start()
 
     def multiply(ch):
-        settle(gathered.at[ch, 1 - c], core_recv.at[2, ch])
+        settle(gathered.at[ch, 1 - c], core_recv.at[1, ch])
         rows = gathered[ch].reshape(total, part_w)
-        wg_copy(ch).wait()
-        gate_acc[...] += jnp.dot(rows, wg[ch], preferred_element_type=F32)
-        wu_copy(ch).wait()
-        up_acc[...] += jnp.dot(rows, wu[ch], preferred_element_type=F32)
+        if ch == 0:
+            settle(w_gate, w_sem.at[1])
+            settle(w_up, w_sem.at[2])
+        product = jnp.dot(rows, wgu[cols(ch), :], preferred_element_type=F32)
+        if ch > 0:
+            product = product + ffn_acc[...]
+        ffn_acc[...] = product
 
     def route():
         router_copy.wait()
@@ -492,7 +531,7 @@
         loop(n, share_start, 1)
         share_in[my_slot] = share_out[...]
 
-    first_stages, first_drain = reduce_scatter(0, attended_part, spread_hidden)
+    first_stages, first_drain = reduce_scatter(attended_part, spread_hidden)
 
     def scoped(f):
         def g(*args):
@@ -501,12 +540,18 @@
 
         return g
 
+    def run(stages, order, after=None):
+        for stage, ch in order:
+            scoped(stages[stage])(ch)
+            if after is not None:
+                after(stage, ch)
+
+    def after_last(stage, ch):
+        if (stage, ch) == (3, CHUNKS - 1):
+            scoped(route)()
+
     with jax.named_scope("merged"):
-        pipeline(
-            [scoped(f) for f in first_stages + (hop_mid, hop_core, multiply)],
-            MERGED,
-            lambda t: pl.when(t == CHUNKS + MERGED[3] - 1)(scoped(route)),
-        )
+        run(first_stages + (hop_mid, hop_core, multiply), MERGED, after_last)
 
     with jax.named_scope("act"):
         settle(share_in.at[pl.ds(0, n - 1)], share_sem.at[1])
@@ -523,30 +568,34 @@
         mine = lax.broadcasted_iota(jnp.int32, share_all.shape, 1) == me // (n // EXPERTS)
         share = jnp.sum(jnp.where(mine, sent, 0.0), axis=1, keepdims=True)
         scale = sent[:, EXPERTS : EXPERTS + 1]
-        gate = gate_acc[...] * scale
-        act[...] = (gate * jax.nn.sigmoid(gate) * up_acc[...] * (scale * share)).astype(BF16)
+        gate = ffn_acc[:, :hidden_units] * scale
+        up = ffn_acc[:, hidden_units:] * (scale * share)
+        act[...] = (gate * jax.nn.sigmoid(gate) * up).astype(BF16)
         first_drain()
 
     def expert_part(ch):
-        wd_copy(ch).wait()
-        return jnp.dot(act[...], wd[ch], preferred_element_type=F32)
+        if ch == 0:
+            settle(wd, w_sem.at[3])
+        return jnp.dot(act[...], wd[:, cols(ch)], preferred_element_type=F32)
 
     def put_out(ch, acc):
         mixed = hid[ch] + acc
         for q in range(seqs):
             out_ref[q, :, cols(ch)] = mixed[q * steps : (q + 1) * steps].astype(BF16)
-
-    second_stages, second_drain = reduce_scatter(1, expert_part, put_out)
+        pltpu.make_async_copy(out_ref.at[:, :, cols(ch)], out_hbm.at[:, :, cols(ch)], out_sem.at[0]).start()
+
+    second_stages, second_drain = reduce_scatter(expert_part, put_out)
     with jax.named_scope("rs2"):
-        pipeline([scoped(f) for f in second_stages], SECOND)
+        run(second_stages, SECOND)
 
     with jax.named_scope("drain"):
         second_drain()
         settle(ctx_in.at[:, pl.ds(0, n - 1)], ctx_send.at[0])
         settle(share_in.at[pl.ds(0, n - 1)], share_sem.at[0])
-        settle(block.at[:, pl.ds(0, LINE - 1)], line_send.at[2])
-        settle(gathered.at[:, 0, pl.ds(0, mids - 1)], mid_send.at[2])
-        settle(gathered.at[:, 0], core_send.at[2])
+        settle(block.at[:, pl.ds(0, LINE - 1)], line_send.at[1])
+        settle(gathered.at[:, 0, pl.ds(0, mids - 1)], mid_send.at[1])
+        settle(gathered.at[:, 0], core_send.at[1])
+        pltpu.make_async_copy(out_ref, out_hbm, out_sem.at[0]).wait()
 
 
 def body(
@@ -588,13 +637,12 @@
         functools.partial(layer_kernel, n),
         out_shape=jax.ShapeDtypeStruct(resid.shape, BF16),
         in_specs=[pl.BlockSpec(memory_space=pltpu.SMEM)] + [hbm] * 13,
-        out_specs=vmem,
+        out_specs=hbm,
         scratch_shapes=[
             pltpu.VMEM(value_up.shape, BF16),
-            pltpu.VMEM((CHUNKS, out_proj.shape[0], part_w), BF16),
-            pltpu.VMEM((CHUNKS, part_w, hidden_units), BF16),
-            pltpu.VMEM((CHUNKS, part_w, hidden_units), BF16),
-            pltpu.VMEM((CHUNKS, hidden_units, part_w), BF16),
+            pltpu.VMEM(out_proj.shape, BF16),
+            pltpu.VMEM((width, 2 * hidden_units), BF16),
+            pltpu.VMEM(w_down.shape, BF16),
             pltpu.VMEM((seqs, kv, cache_kv.shape[1]), BF16),
             pltpu.VMEM((seqs, LANES, kv), BF16),
             pltpu.VMEM((seqs, steps * heads, kv), BF16),
@@ -611,31 +659,31 @@
             pltpu.VMEM((n * steps * heads_per, LAT), F32),
             pltpu.VMEM((total, value_up.shape[1]), BF16),
             pltpu.VMEM((total, hidden_units), BF16),
-            pltpu.VMEM((total, hidden_units), F32),
-            pltpu.VMEM((total, hidden_units), F32),
+            pltpu.VMEM((total, 2 * hidden_units), F32),
             pltpu.VMEM((CHUNKS, toks, part_w), F32),
             pltpu.VMEM((CHUNKS, CORES, mids, group, part_w), BF16),
             pltpu.VMEM((CHUNKS, mids, group, part_w), BF16),
             pltpu.VMEM((CHUNKS, LINE, toks, part_w), BF16),
-            *landing,
             *landing,
             pltpu.VMEM((CHUNKS, LINE, toks, part_w), BF16),
             pltpu.VMEM((CHUNKS, CORES, mids, group, part_w), BF16),
             pltpu.VMEM((toks, LANES), F32),
             pltpu.VMEM((n, toks, LANES), F32),
             pltpu.VMEM((total, LANES), F32),
-            dma((4, CHUNKS)),
+            pltpu.VMEM(resid.shape, BF16),
+            dma((1,)),
+            dma((4,)),
             dma((7,)),
             dma((seqs, KEY_BLOCKS + 1)),
             dma((1,)),
             dma((seqs,)),
             dma((2,)),
-            dma((3,)),
-            dma((3, CHUNKS)),
-            dma((3,)),
-            dma((3, CHUNKS)),
-            dma((3,)),
-            dma((3, CHUNKS)),
+            dma((2,)),
+            dma((2, CHUNKS)),
+            dma((2,)),
+            dma((2, CHUNKS)),
+            dma((2,)),
+            dma((2, CHUNKS)),
         ],
         compiler_params=pltpu.CompilerParams(
             collective_id=0, has_side_effects=True, vmem_limit_bytes=67043328

time: 57.1 us -> 54.9 us (0.961)
  Pallas kernels: 55.5 us -> 53.2 us
    pallas_call x1, Pallas kernels: 55.5 us -> 53.2 us  [body(): pl.pallas_call(functools.partial(layer_kernel, n), out_shape=jax.ShapeDty...]
where the time goes in v2:
time: 54.9 us; the launch traced here: 54.7 us
  Pallas kernels  53.2 us (97%)
  local copies, waits for them, and re-layouts  1.48 us (3%)
    pallas_call x1, Pallas kernels, body(): pl.pallas_call(functools.partial(layer_kernel, n), out_shape=jax.ShapeDty...  53.2 us
    unnamed x1, local copies, waits for them, and re-layouts  1.48 us

profile of v2, /device:TPU:0, one launch (start us, length us, event | category | flops | bytes accessed | tf_op | source)
XLA Modules:
  0.0 54.7 jit_solution(3033797981223310672)
XLA Ops:
  0.0 53.2 %shard_map.136 = bf16[2,2,7168]{2,1,0:T(2,128)(2,1)} custom-call(s32[2]{0:T(128)} %len_ref.1, bf16[2,2,576]{2,1,0:T(2,128)(2,1)} %new_hbm.1, bf16[56,128]{1,0:T(8,128)(2,1)} %bitcast.9, bf16[16,7168]{1,0:T(8,128)(2,1)} %bitcast.8, s32[4,8]{1,0:T(4,128)} %bitcast.10, s32[4,8]{1,0:T(4,128)} %bitcast.11, bf16[2,576,2048]{2,1,0:T(8,128)(2,1)} %bitcast.6, ...), custom_call_target="tpu_custom_call" | custom-call | tf_op jit(solution)/shard_map/pallas_call | solution.py:636
  53.2 1.5 %copy.16 = bf16[2,2,7168]{2,1,0:T(2,128)(2,1)} copy(bf16[2,2,7168]{2,1,0:T(2,128)(2,1)} %shard_map.136) | data formatting | bytes 114688
